TPU v7x, 32 devices: a whole 2x2x4 slice. The times are simulated.
32 devices in a mesh: ctx: 8 (over z, y), fsdp: 4 (over x, core).
Axes of the slice: x: 2, y: 2, z: 4, core: 2. Of those that a mesh axis runs over, the one named last changes fastest.
Arguments:
- tokens: bfloat16 [4, 1024, 1600], P('fsdp', 'ctx'), may hold values from -6 to 6
- block_order: int32 [4, 16], P('fsdp'), may hold values from 0 to 15, each once within a row
- qkv_weight: bfloat16 [1600, 4800], P('fsdp'), may hold values from -0.15625 to 0.15625
- query_bias: float32 [1600], replicated, may hold values from -3 to 3
- value_bias: float32 [1600], replicated, may hold values from -0.18 to 0.18
- out_weight: bfloat16 [1600, 1600], P('fsdp'), may hold values from -2.5 to 2.5
- out_bias: float32 [1600], replicated, may hold values from -1.8 to 1.8
- expand_weight: bfloat16 [1600, 6400], P('fsdp'), may hold values from -0.15625 to 0.15625
- expand_bias: float32 [6400], replicated, may hold values from -3 to 3
- shrink_weight: bfloat16 [6400, 1600], P('fsdp'), may hold values from -0.078125 to 0.078125
- shrink_bias: float32 [1600], replicated, may hold values from -1.8 to 1.8
- first_gain: float32 [1600], replicated, may hold values from 0.5 to 1.5
- first_shift: float32 [1600], replicated, may hold values from -1.8 to 1.8
- second_gain: float32 [1600], replicated, may hold values from 0.5 to 1.5
- second_shift: float32 [1600], replicated, may hold values from -1.8 to 1.8
- cotangent: bfloat16 [4, 1024, 1600], P('fsdp', 'ctx'), may hold values from -6 to 6
Outputs:
- result: bfloat16 [4, 1024, 1600], P('fsdp', 'ctx')
- grad_tokens: float32 [4, 1024, 1600], P('fsdp', 'ctx')
- grad_qkv: float32 [1600, 4800], P('fsdp', 'ctx')
- grad_outw: float32 [1600, 1600], P('fsdp', 'ctx')
- grad_expand: float32 [1600, 6400], P('fsdp', 'ctx')
- grad_shrink: float32 [6400, 1600], P('fsdp', 'ctx')
- grad_query_bias: float32 [1600], replicated
- grad_value_bias: float32 [1600], replicated
- grad_out_bias: float32 [1600], replicated
- grad_expand_bias: float32 [6400], replicated
- grad_shrink_bias: float32 [1600], replicated
- grad_first_gain: float32 [1600], replicated
- grad_first_shift: float32 [1600], replicated
- grad_second_gain: float32 [1600], replicated
- grad_second_shift: float32 [1600], replicated
Inputs may be any that keep to these rules, and one draw needn't show every extreme that they name: Each row of block_order names every block of its sequence once.
All inputs are finite; a program needn't handle non-finite values.
Results may differ from a plain program's by a relative error of at most 0.015.
Values may be sent and summed in bfloat16 or wider, within the bound.
A program may use at most 384 MiB of HBM per device.

v0:
```python
import jax
import jax.numpy as jnp
from jax import lax
from jax.sharding import PartitionSpec as P

HEADS = 25
HEAD_DIM = 64
EPSILON = 1e-05


def layer_norm(values, gain, shift):
    center = jnp.mean(values, axis=-1, keepdims=True)
    centred = values - center
    spread = jnp.mean(centred * centred, axis=-1, keepdims=True)
    return centred * lax.rsqrt(spread + EPSILON) * gain + shift


def smooth_gelu(values):
    return (
        0.5
        * values
        * (1.0 + jnp.tanh(0.7978845608028654 * (values + 0.044715 * values * values * values)))
    )


def fetch(weight):
    return lax.all_gather(weight, "fsdp", axis=0, tiled=True)


def against(left, weight):
    return lax.dot_general(
        left, weight, (((1,), (1,)), ((), ())), preferred_element_type=jnp.float32
    )


def shard_rows(local):
    return lax.psum_scatter(
        local.astype(jnp.bfloat16), "fsdp", scatter_dimension=0, tiled=True
    ).astype(jnp.float32)


def column_grad(left, right):
    whole_left = lax.all_gather(left, "ctx", axis=0, tiled=True)
    right_columns = lax.all_to_all(right, "ctx", split_axis=1, concat_axis=0, tiled=True)
    local = lax.dot_general(
        whole_left, right_columns, (((0,), (0,)), ((), ())), preferred_element_type=jnp.float32
    )
    return shard_rows(local)


def shared_grad(left, right):
    return column_grad(left, right)


def masked_scores(queries, query_pos, keys, key_pos, factor):
    scores = jnp.einsum("qhd,khd->hqk", queries, keys, preferred_element_type=jnp.float32) * factor
    allowed = (key_pos[None, :] <= query_pos[:, None])[None]
    return jnp.where(allowed, scores, -jnp.inf)


def body(
    tokens,
    block_order,
    qkv_weight,
    query_bias,
    value_bias,
    out_weight,
    out_bias,
    expand_weight,
    expand_bias,
    shrink_weight,
    shrink_bias,
    first_gain,
    first_shift,
    second_gain,
    second_shift,
    cotangent,
):
    inputs = tokens[0].astype(jnp.float32)
    rows = inputs.shape[0]
    width = inputs.shape[1]
    half = rows // 2
    factor = HEAD_DIM ** (-0.5)
    place = lax.axis_index("ctx")
    key_pos = (block_order[0][:, None] * half + jnp.arange(half, dtype=jnp.int32)[None, :]).reshape(
        -1
    )
    length = key_pos.shape[0]
    query_pos = lax.dynamic_slice_in_dim(key_pos, place * rows, rows)
    block = min(512, length)
    count = length // block
    normed_one = layer_norm(inputs, first_gain, first_shift)
    lowered_one = normed_one.astype(jnp.bfloat16)
    project = jnp.dot(lowered_one, fetch(qkv_weight), preferred_element_type=jnp.float32)
    query = (project[:, :width] + query_bias).astype(jnp.bfloat16)
    keys_own = project[:, width : 2 * width].astype(jnp.bfloat16)
    values_own = (project[:, 2 * width :] + value_bias).astype(jnp.bfloat16)
    all_keys, all_values = (
        lax.all_gather(keys_own, "ctx", axis=0, tiled=True),
        lax.all_gather(values_own, "ctx", axis=0, tiled=True),
    )
    query_heads = query.reshape(rows, HEADS, HEAD_DIM)
    key_blocks = all_keys.reshape(count, block, HEADS, HEAD_DIM)
    value_blocks = all_values.reshape(count, block, HEADS, HEAD_DIM)
    pos_blocks = key_pos.reshape(count, block)

    def running(carry, pieces):
        highest, total = carry
        key_piece, pos_piece = pieces
        scores = masked_scores(query_heads, query_pos, key_piece, pos_piece, factor)
        fresh = jnp.maximum(highest, jnp.max(scores, axis=-1))
        total = total * jnp.exp(highest - fresh) + jnp.sum(
            jnp.exp(scores - fresh[..., None]), axis=-1
        )
        return ((fresh, total), None)

    start = (jnp.full((HEADS, rows), -1e30, jnp.float32), jnp.zeros((HEADS, rows), jnp.float32))
    (highest, total), unused = lax.scan(running, start, (key_blocks, pos_blocks))
    log_sum = highest + jnp.log(total)

    def weighted(acc, pieces):
        key_piece, value_piece, pos_piece = pieces
        scores = masked_scores(query_heads, query_pos, key_piece, pos_piece, factor)
        probs = jnp.exp(scores - log_sum[..., None]).astype(jnp.bfloat16)
        return (
            acc
            + jnp.einsum("hqk,khd->qhd", probs, value_piece, preferred_element_type=jnp.float32),
            None,
        )

    attended_heads, unused = lax.scan(
        weighted,
        jnp.zeros((rows, HEADS, HEAD_DIM), jnp.float32),
        (key_blocks, value_blocks, pos_blocks),
    )
    attended = attended_heads.reshape(rows, width)
    attended_low = attended.astype(jnp.bfloat16)
    middle = (
        inputs
        + jnp.dot(attended_low, fetch(out_weight), preferred_element_type=jnp.float32)
        + out_bias
    )
    normed_two = layer_norm(middle, second_gain, second_shift)
    lowered_two = normed_two.astype(jnp.bfloat16)
    expanded = (
        jnp.dot(lowered_two, fetch(expand_weight), preferred_element_type=jnp.float32) + expand_bias
    )
    hidden_low = smooth_gelu(expanded).astype(jnp.bfloat16)
    shrink_full = fetch(shrink_weight)
    result = (
        middle + jnp.dot(hidden_low, shrink_full, preferred_element_type=jnp.float32) + shrink_bias
    )
    grad_low = cotangent[0]
    grad_result = grad_low.astype(jnp.float32)
    grad_shrink = shared_grad(hidden_low, grad_low)
    grad_shrink_bias = jnp.sum(grad_result, axis=0)
    grad_hidden = against(grad_low, shrink_full)
    unused, gelu_back = jax.vjp(smooth_gelu, expanded)
    (grad_expanded,) = gelu_back(grad_hidden)
    expanded_low = grad_expanded.astype(jnp.bfloat16)
    grad_expand_bias = jnp.sum(expanded_low.astype(jnp.float32), axis=0)
    grad_expand = shared_grad(lowered_two, expanded_low)
    grad_normed_two = against(expanded_low, fetch(expand_weight))
    unused, second_back = jax.vjp(layer_norm, middle, second_gain, second_shift)
    grad_middle_norm, grad_second_gain, grad_second_shift = second_back(grad_normed_two)
    grad_middle = grad_result + grad_middle_norm
    middle_low = grad_middle.astype(jnp.bfloat16)
    grad_out_bias = jnp.sum(middle_low.astype(jnp.float32), axis=0)
    grad_outw = shared_grad(attended_low, middle_low)
    grad_att_low = against(middle_low, fetch(out_weight)).astype(jnp.bfloat16)
    grad_att_heads = grad_att_low.reshape(rows, HEADS, HEAD_DIM)
    delta = jnp.sum(grad_att_heads.astype(jnp.float32) * attended_heads, axis=-1).T

    def key_step(acc, pieces):
        key_piece, value_piece, pos_piece = pieces
        scores = masked_scores(query_heads, query_pos, key_piece, pos_piece, factor)
        probs = jnp.exp(scores - log_sum[..., None])
        slopes = jnp.einsum(
            "qhd,khd->hqk", grad_att_heads, value_piece, preferred_element_type=jnp.float32
        )
        score_grad = (probs * (slopes - delta[..., None])).astype(jnp.bfloat16)
        acc = acc + jnp.einsum(
            "hqk,khd->qhd", score_grad, key_piece, preferred_element_type=jnp.float32
        )
        return (acc, (probs.astype(jnp.bfloat16), score_grad))

    empty_heads = jnp.zeros((rows, HEADS, HEAD_DIM), jnp.float32)

    def query_step(acc, pieces):
        acc, unused_pair = key_step(acc, pieces)
        return (acc, None)

    query_acc, unused = lax.scan(query_step, empty_heads, (key_blocks, value_blocks, pos_blocks))
    all_queries, all_grads = (
        lax.all_gather(query, "ctx", axis=0, tiled=True),
        lax.all_gather(grad_att_low, "ctx", axis=0, tiled=True),
    )
    all_sums, all_deltas = (
        lax.all_gather(log_sum.T, "ctx", axis=0, tiled=True),
        lax.all_gather(delta.T, "ctx", axis=0, tiled=True),
    )
    own_keys = keys_own.reshape(rows, HEADS, HEAD_DIM)
    own_values = values_own.reshape(rows, HEADS, HEAD_DIM)

    def owner_step(carry, pieces):
        key_acc, value_acc = carry
        query_piece, grad_piece, sum_piece, delta_piece, pos_piece = pieces
        scores = masked_scores(query_piece, pos_piece, own_keys, query_pos, factor)
        probs = jnp.exp(scores - sum_piece.T[..., None])
        slopes = jnp.einsum(
            "qhd,khd->hqk", grad_piece, own_values, preferred_element_type=jnp.float32
        )
        score_grad = (probs * (slopes - delta_piece.T[..., None])).astype(jnp.bfloat16)
        key_acc = key_acc + jnp.einsum(
            "hqk,qhd->khd", score_grad, query_piece, preferred_element_type=jnp.float32
        )
        value_acc = value_acc + jnp.einsum(
            "hqk,qhd->khd",
            probs.astype(jnp.bfloat16),
            grad_piece,
            preferred_element_type=jnp.float32,
        )
        return ((key_acc, value_acc), None)

    (key_acc, value_acc), unused = lax.scan(
        owner_step,
        (empty_heads, empty_heads),
        (
            all_queries.reshape(count, block, HEADS, HEAD_DIM),
            all_grads.reshape(count, block, HEADS, HEAD_DIM),
            all_sums.reshape(count, block, HEADS),
            all_deltas.reshape(count, block, HEADS),
            pos_blocks,
        ),
    )
    grad_keys = key_acc.reshape(rows, width)
    grad_values = value_acc.reshape(rows, width)
    grad_query_low = (query_acc.reshape(rows, width) * factor).astype(jnp.bfloat16)
    grad_key_low = (grad_keys * factor).astype(jnp.bfloat16)
    grad_value_low = grad_values.astype(jnp.bfloat16)
    project_grad = jnp.concatenate([grad_query_low, grad_key_low, grad_value_low], axis=1)
    grad_query_bias = jnp.sum(grad_query_low.astype(jnp.float32), axis=0)
    grad_value_bias = jnp.sum(grad_value_low.astype(jnp.float32), axis=0)
    grad_qkv = shared_grad(lowered_one, project_grad)
    grad_normed_one = against(project_grad, fetch(qkv_weight))
    unused, first_back = jax.vjp(layer_norm, inputs, first_gain, first_shift)
    grad_first_input, grad_first_gain, grad_first_shift = first_back(grad_normed_one)
    grad_inputs = grad_middle + grad_first_input
    summed = lax.psum(
        (
            grad_query_bias,
            grad_value_bias,
            grad_out_bias,
            grad_expand_bias,
            grad_shrink_bias,
            grad_first_gain,
            grad_first_shift,
            grad_second_gain,
            grad_second_shift,
        ),
        ("ctx", "fsdp"),
    )
    return (
        result.astype(jnp.bfloat16)[None],
        grad_inputs[None],
        grad_qkv,
        grad_outw,
        grad_expand,
        grad_shrink,
        summed[0],
        summed[1],
        summed[2],
        summed[3],
        summed[4],
        summed[5],
        summed[6],
        summed[7],
        summed[8],
    )


def solution(mesh):
    placed = (
        P("fsdp", "ctx", None),
        P("fsdp", None),
        P("fsdp", None),
        P(),
        P(),
        P("fsdp", None),
        P(),
        P("fsdp", None),
        P(),
        P("fsdp", None),
        P(),
        P(),
        P(),
        P(),
        P(),
        P("fsdp", "ctx", None),
    )
    return jax.shard_map(
        body,
        mesh=mesh,
        in_specs=placed,
        out_specs=(
            P("fsdp", "ctx", None),
            P("fsdp", "ctx", None),
            P("fsdp", "ctx"),
            P("fsdp", "ctx"),
            P("fsdp", "ctx"),
            P("fsdp", "ctx"),
            P(),
            P(),
            P(),
            P(),
            P(),
            P(),
            P(),
            P(),
            P(),
        ),
        check_vma=False,
    )
```

profile of v0, /device:TPU:8, one launch (start us, length us, event | category | flops | bytes accessed | tf_op | source)
XLA Modules:
  0.0 1413.1 jit_solution(10884619457395824276)
XLA Ops:
  9.8 100.0 %all-gather.13.cloned.1.call-done = bf16[1600,4800]{1,0:T(8,128)(2,1)} async-done(((bf16[400,4800]{1,0:T(8,128)(2,1)}), bf16[1600,4800]{1,0:T(8,128)(2,1)}) %all-gather.13.cloned.1.call-update) | async-done | bytes 15360016 | tf_op jit(solution)/shard_map/all_gather | solution.py:27
  109.8 9.6 fusion.172
  125.1 57.6 %all-gather.17.cloned.1.call-done = bf16[1024,1600]{0,1:T(8,128)(2,1)} async-done(((bf16[128,1600]{0,1:T(8,128)(2,1)}), bf16[1024,1600]{0,1:T(8,128)(2,1)}) %all-gather.17.cloned.1.call-update) | async-done | bytes 3276816 | tf_op jit(solution)/shard_map/all_gather | solution.py:99
  182.7 8.5 reshape.298
  191.2 2.7 copy.79
  193.9 53.8 %all-gather.15.cloned.1.call-done = bf16[1024,1600]{0,1:T(8,128)(2,1)} async-done(((bf16[128,1600]{0,1:T(8,128)(2,1)}), bf16[1024,1600]{0,1:T(8,128)(2,1)}) %all-gather.15.cloned.1.call-update) | async-done | bytes 3276816 | tf_op jit(solution)/shard_map/all_gather | solution.py:100
  247.7 8.5 reshape.297
  256.2 4.9 copy.78
  261.0 19.3 %while.48 = (s32[]{:T(128)}, f32[25,128]{1,0:T(8,128)S(1)}, f32[25,128]{1,0:T(8,128)S(1)}, s32[2,512]{1,0:T(2,128)S(1)}, s32[128]{0:T(128)S(1)}, /*index=5*/bf16...) while((s32[]{:T(128)}, f32[25,128]{1,0:T(8,128)S(1)}, ...), condition=%wide.region_5.6_spmd.clone, body=%wide.region_2.5_spmd.clone.sunk | while | flops 221265536 | bytes 15524976 | solution.py:118
  261.2 5.2 fusion.228
  266.4 4.3 exponential_reduce_fusion.2
  270.9 5.2 fusion.228
  276.1 4.2 exponential_reduce_fusion.2
  280.4 10.0 while.49
  280.5 4.7 fusion.234
  285.4 5.0 fusion.234
  292.5 5.0 fusion.171
  300.1 120.2 %all-gather.21.cloned.1.call-done = bf16[1600,6400]{1,0:T(8,128)(2,1)} async-done(((bf16[400,6400]{1,0:T(8,128)(2,1)}), bf16[1600,6400]{1,0:T(8,128)(2,1)}) %all-gather.21.cloned.1.call-update) | async-done | bytes 20480016 | tf_op jit(solution)/shard_map/all_gather | solution.py:27
  420.3 14.0 multiply_convert_fusion.6
  434.3 120.9 %all-gather.23.cloned.1.call-done = bf16[6400,1600]{1,0:T(8,128)(2,1)} async-done(((bf16[1600,1600]{1,0:T(8,128)(2,1)}), bf16[6400,1600]{1,0:T(8,128)(2,1)}) %all-gather.23.cloned.1.call-update) | async-done | bytes 20480016 | tf_op jit(solution)/shard_map/all_gather | solution.py:27
  555.2 12.3 convert_reduce_fusion
  567.5 12.8 multiply_reduce_fusion
  583.2 2.3 convolution_convert_fusion.4
  586.9 6.1 all-to-all-start.1
  593.0 42.4 %all_gather.52 = f32[1024,25]{0,1:T(8,128)S(1)} all-gather(f32[128,25]{0,1:T(8,128)S(1)} %bitcast.354), channel_id=1, replica_groups=mesh['ctx'=8,'fsdp'=4] {'ctx'}, dimensions={0}, use_global_device_ids=true | all-gather | bytes 115200 | tf_op jit(solution)/shard_map/all_gather | solution.py:199
  636.1 8.5 reshape.301
  644.6 4.4 copy.82
  649.0 3.7 copy.88
  654.1 8.4 all-to-all-start.2
  662.5 58.5 %all-gather.31.cloned.1.call-done = bf16[1024,1600]{0,1:T(8,128)(2,1)} async-done(((bf16[128,1600]{0,1:T(8,128)(2,1)}), bf16[1024,1600]{0,1:T(8,128)(2,1)}) %all-gather.31.cloned.1.call-update) | async-done | bytes 3276816 | tf_op jit(solution)/shard_map/all_gather | solution.py:43
  721.0 3.9 convolution_convert_fusion.3
  725.0 24.6 %while.50 = (s32[]{:T(128)}, f32[128,25,64]{0,2,1:T(8,128)}, bf16[2,512,25,64]{1,3,2,0:T(8,128)(2,1)S(1)}, s32[2,512]{1,0:T(2,128)S(1)}, s32[128]{0:T(128)S(1)},...) while((s32[]{:T(128)}, f32[128,25,64]{0,2,1:T(8,128)}, ...), condition=%wide.region_14.15_spmd.clone, body=%wide.region_13.14_spmd.clone.sunk | while | flops 639451136 | bytes 20651656 | solution.py:193
  725.0 4.8 fusion.241
  729.9 7.3 fusion.242
  737.2 4.8 fusion.241
  742.2 7.4 fusion.242
  749.6 29.6 %all_gather.54 = f32[1024,25]{0,1:T(8,128)S(1)} all-gather(f32[128,25]{0,1:T(8,128)S(1)} %bitcast.353), channel_id=1, replica_groups=mesh['ctx'=8,'fsdp'=4] {'ctx'}, dimensions={0}, use_global_device_ids=true | all-gather | bytes 115200 | tf_op jit(solution)/shard_map/all_gather | solution.py:200
  782.0 3.9 all-gather.33.cloned.1.call-done
  785.8 7.6 convolution_convert_fusion.1
  793.4 56.4 %all-gather.27.cloned.1.call-done = bf16[1024,1600]{0,1:T(8,128)(2,1)} async-done(((bf16[128,1600]{0,1:T(8,128)(2,1)}), bf16[1024,1600]{0,1:T(8,128)(2,1)}) %all-gather.27.cloned.1.call-update) | async-done | bytes 3276816 | tf_op jit(solution)/shard_map/all_gather | solution.py:196
  849.9 8.7 reshape.304
  858.6 4.8 copy.84
  863.4 41.6 %while.51 = (s32[]{:T(128)}, f32[128,25,64]{0,2,1:T(8,128)}, f32[128,25,64]{0,2,1:T(8,128)}, bf16[2,512,25,64]{1,3,2,0:T(8,128)(2,1)S(1)}, s32[128]{0:T(128)S(1)...) while((s32[]{:T(128)}, f32[128,25,64]{0,2,1:T(8,128)}, ...), condition=%wide.region_16.17_spmd.clone, body=%wide.region_15.16_spmd.clone.sunk | while | flops 856129536 | bytes 31107220 | solution.py:225
  863.4 4.8 fusion.250
  869.4 9.0 fusion.251
  878.4 5.6 fusion.252
  884.0 4.8 fusion.250
  890.0 9.2 fusion.251
  899.2 5.8 fusion.252
  906.7 2.1 pad_maximum_fusion
  908.8 5.8 all-to-all-start
  914.6 48.3 %all-to-all-done = bf16[128,8,600]{0,2,1:T(8,128)(2,1)S(1)} async-done(((bf16[128,8,600]{0,2,1:T(8,128)(2,1)}), bf16[128,8,600]{0,2,1:T(8,128)(2,1)S(1)}, u32[]{:S(2)}, u32[]{:S(2)}) %all-to-all-start) | async-done | bytes 1228832 | tf_op jit(solution)/shard_map/all_to_all | solution.py:44
  962.9 6.0 convolution_convert_fusion.2
  969.0 29.7 %all_to_all.76 = bf16[128,8,200]{0,2,1:T(8,128)(2,1)S(1)} all-to-all(bf16[128,8,200]{0,2,1:T(8,128)(2,1)S(1)} %bitcast.332), channel_id=1, replica_groups=mesh['ctx'=8,'fsdp'=4] {'ctx'}, dimensions={1} | all-to-all | bytes 819200 | tf_op jit(solution)/shard_map/all_to_all | solution.py:44
  998.7 120.4 %all-gather.35.cloned.1.call-done = bf16[1024,6400]{1,0:T(8,128)(2,1)} async-done(((bf16[128,6400]{1,0:T(8,128)(2,1)}), bf16[1024,6400]{1,0:T(8,128)(2,1)}) %all-gather.35.cloned.1.call-update) | async-done | bytes 13107216 | tf_op jit(solution)/shard_map/all_gather | solution.py:43
  1119.1 9.0 convolution_convert_fusion
  1128.1 4.8 copy.93
  1134.3 9.7 fusion.168
  1147.2 13.3 fusion.136
  1162.2 21.4 %reduce-scatter.11.cloned.1.call-done = bf16[400,800]{1,0:T(8,128)(2,1)} async-done(((bf16[1600,800]{1,0:T(8,128)(2,1)}), bf16[400,800]{1,0:T(8,128)(2,1)}) %reduce-scatter.11.cloned.1.call-update) | async-done | bytes 640016 | tf_op jit(solution)/shard_map/reduce_scatter | solution.py:37
  1183.6 2.3 convert_element_type.142
  1185.9 31.0 %reduce-scatter.7.cloned.1.call-done = bf16[400,600]{1,0:T(8,128)(2,1)} async-done(((bf16[1600,600]{1,0:T(8,128)(2,1)}), bf16[400,600]{1,0:T(8,128)(2,1)}) %reduce-scatter.7.cloned.1.call-update) | async-done | bytes 480016 | tf_op jit(solution)/shard_map/reduce_scatter | solution.py:37
  1219.0 39.1 %reduce-scatter.13.cloned.1.call-done = bf16[1600,200]{1,0:T(8,128)(2,1)} async-done(((bf16[6400,200]{1,0:T(8,128)(2,1)}), bf16[1600,200]{1,0:T(8,128)(2,1)}) %reduce-scatter.13.cloned.1.call-update) | async-done | bytes 640016
  1260.8 133.7 %all-reduce.3.cloned.1.call-done = (f32[1600]{0:T(1024)}, f32[1600]{0:T(1024)}, f32[1600]{0:T(1024)}, f32[6400]{0:T(1024)}, f32[1600]{0:T(1024)}, /*index=5*/f32...) async-done(((f32[1600]{0:T(1024)}, f32[1600]{0:T(1024)}, f32[1600]{0:T(1024)}, f32[6400]{0:T(1024)}, f32[1600]{0:T(1024)}, /*index=5*/f32[1600]{0:T(1024)}, ...) | async-done | bytes 76816 | tf_op jit(solution)/shard_map/psum | solution.py:249
  (194 shorter events, 49.7 us)
Async XLA Ops:
  7.2 1.0 copy-start.4
  7.2 2.0 copy-start.16
  7.2 2.0 copy-start.21
  7.2 102.6 %all-gather.13.cloned.1.call-start = ((), (), s32[]{:S(2)}) async-start(), calls=%async_computation.8 | async-start | bytes 19456000 | tf_op jit(solution)/shard_map/all_gather | solution.py:27
  7.9 174.7 %all-gather.17.cloned.1.call-start = ((), (), s32[]{:S(2)}) async-start(), calls=%async_computation.10 | async-start | bytes 3686400 | tf_op jit(solution)/shard_map/all_gather | solution.py:99
  8.4 1.3 copy-start.19
  8.7 0.5 copy-start.29
  9.2 0.6 copy-start.27
  9.7 109.7 %copy-start.12 = (bf16[128,1600]{0,1:T(8,128)(2,1)}, bf16[128,1600]{0,1:T(8,128)(2,1)S(1)}, u32[]{:S(2)}) copy-start(bf16[128,1600]{0,1:T(8,128)(2,1)S(1)} %fusion.149) | copy-start | bytes 1228804
  9.8 110.5 %copy-start.22 = (f32[1600]{0:T(1024)S(1)}, f32[1600]{0:T(1024)}, u32[]{:S(2)}) copy-start(f32[1600]{0:T(1024)} %param.27) | copy-start | bytes 19204
  9.8 110.5 %copy-start.23 = (f32[1600]{0:T(1024)S(1)}, f32[1600]{0:T(1024)}, u32[]{:S(2)}) copy-start(f32[1600]{0:T(1024)} %param.28) | copy-start | bytes 19204
  120.2 127.5 %all-gather.15.cloned.1.call-start = ((), (), s32[]{:S(2)}) async-start(), calls=%async_computation.9 | async-start | bytes 3686400 | tf_op jit(solution)/shard_map/all_gather | solution.py:100
  121.7 170.8 %all-gather.19.cloned.1.call-start = ((), (), s32[]{:S(2)}) async-start(), calls=%async_computation.11 | async-start | bytes 6656000 | tf_op jit(solution)/shard_map/all_gather | solution.py:27
  122.3 298.1 %all-gather.21.cloned.1.call-start = ((), (), s32[]{:S(2)}) async-start(), calls=%async_computation.12 | async-start | bytes 25600000 | tf_op jit(solution)/shard_map/all_gather | solution.py:27
  122.9 1.6 copy-start.31
  122.9 432.3 %all-gather.23.cloned.1.call-start = ((), (), s32[]{:S(2)}) async-start(), calls=%async_computation.13 | async-start | bytes 26624000 | tf_op jit(solution)/shard_map/all_gather | solution.py:27
  123.4 512.6 %all-gather.25.cloned.1.call-start = ((), (), s32[]{:S(2)}) async-start(), calls=%async_computation.14 | async-start | bytes 3686400 | tf_op jit(solution)/shard_map/all_gather | solution.py:195
  124.2 596.8 %all-gather.31.cloned.1.call-start = ((), (), s32[]{:S(2)}) async-start(), calls=%async_computation.18 | async-start | bytes 3686400 | tf_op jit(solution)/shard_map/all_gather | solution.py:43
  280.4 12.1 copy-start.24
  292.4 6.0 copy-start.15
  292.4 6.0 copy-start.25
  292.4 127.9 %copy-start.18 = (f32[6400]{0:T(1024)S(1)}, f32[6400]{0:T(1024)}, u32[]{:S(2)}) copy-start(f32[6400]{0:T(1024)} %param.32) | copy-start | bytes 76804
  292.4 493.4 %all-gather.33.cloned.1.call-start = ((), (), s32[]{:S(2)}) async-start(), calls=%async_computation.20 | async-start | bytes 3686400 | tf_op jit(solution)/shard_map/all_gather | solution.py:43
  297.4 0.9 copy-start.1
  299.6 550.2 %all-gather.27.cloned.1.call-start = ((), (), s32[]{:S(2)}) async-start(), calls=%async_computation.15 | async-start | bytes 3686400 | tf_op jit(solution)/shard_map/all_gather | solution.py:196
  555.2 12.3 copy-start.2
  567.5 12.8 copy-start.7
  567.5 15.8 %slice-start = ((s8[5324800]{0:T(1024)(128)(4,1)}), s8[4194304]{0:T(1024)(128)(4,1)S(1)}, s32[]{:S(2)}) async-start(s8[5324800]{0:T(1024)(128)(4,1)} %bitcast.330), calls=%async_computation.25 | async-start | bytes 8388608
  567.5 14.1 copy-start.10
  567.5 15.8 %slice-start.1 = ((s8[5324800]{0:T(1024)(128)(4,1)}), s8[1130496]{0:T(1024)(128)(4,1)S(1)}, s32[]{:S(2)}) async-start(s8[5324800]{0:T(1024)(128)(4,1)} %bitcast.330), calls=%async_computation.26 | async-start | bytes 2260992
  580.6 1.0 copy-start.8
  582.5 0.7 copy-start.14
  585.6 329.0 %all-gather.29.cloned.1.call-start = ((), (), s32[]{:S(2)}) async-start(), calls=%async_computation.16 | async-start | bytes 3686400 | tf_op jit(solution)/shard_map/all_gather | solution.py:43
  586.3 532.7 %all-gather.35.cloned.1.call-start = ((), (), s32[]{:S(2)}) async-start(), calls=%async_computation.22 | async-start | bytes 14745600 | tf_op jit(solution)/shard_map/all_gather | solution.py:43
  586.9 67.2 %all-to-all-start.1 = ((bf16[128,8,200]{0,2,1:T(8,128)(2,1)}), bf16[128,8,200]{0,2,1:T(8,128)(2,1)}, u32[]{:S(2)}, u32[]{:S(2)}) async-start(bf16[128,8,200]{0,2,1:T(8,128)(2,1)} %bitcast.347), calls=%async_computation.2 | async-start | bytes 819200 | tf_op jit(solution)/shard_map/all_to_all | solution.py:44
  654.1 127.9 %all-to-all-start.2 = ((bf16[128,8,800]{0,2,1:T(8,128)(2,1)}), bf16[128,8,800]{0,2,1:T(8,128)(2,1)}, u32[]{:S(2)}, u32[]{:S(2)}) async-start(bf16[128,8,800]{0,2,1:T(8,128)(2,1)} %bitcast.329), calls=%async_computation.4 | async-start | bytes 3276800 | tf_op jit(solution)/shard_map/all_to_all | solution.py:44
  662.5 498.1 %reduce-scatter.9.cloned.1.call-start = ((), (), s32[]{:S(2)}) async-start(), calls=%async_computation.19 | async-start | bytes 1024000 | tf_op jit(solution)/shard_map/reduce_scatter | solution.py:37
  724.9 458.7 %reduce-scatter.11.cloned.1.call-start = ((), (), s32[]{:S(2)}) async-start(), calls=%async_computation.21 | async-start | bytes 3584000 | tf_op jit(solution)/shard_map/reduce_scatter | solution.py:37
  858.6 4.8 copy-start
  908.8 54.1 %all-to-all-start = ((bf16[128,8,600]{0,2,1:T(8,128)(2,1)}), bf16[128,8,600]{0,2,1:T(8,128)(2,1)S(1)}, u32[]{:S(2)}, u32[]{:S(2)}) async-start(bf16[128,8,600]{0,2,1:T(8,128)(2,1)} %bitcast.15), calls=%async_computation | async-start | bytes 2457600 | tf_op jit(solution)/shard_map/all_to_all | solution.py:44
  914.6 54.4 %copy-start.11 = (bf16[1,128,1600]{1,2,0:T(8,128)(2,1)S(1)}, bf16[1,128,1600]{1,2,0:T(8,128)(2,1)}, u32[]{:S(2)}) copy-start(bf16[1,128,1600]{1,2,0:T(8,128)(2,1)} %param.39) | copy-start | bytes 1228804
  914.6 302.4 %reduce-scatter.7.cloned.1.call-start = ((), (), s32[]{:S(2)}) async-start(), calls=%async_computation.17 | async-start | bytes 2560000 | tf_op jit(solution)/shard_map/reduce_scatter | solution.py:37
  968.9 289.2 %reduce-scatter.13.cloned.1.call-start = ((), (), s32[]{:S(2)}) async-start(), calls=%async_computation.23 | async-start | bytes 4096000
  1128.1 6.2 copy-start.5
  1128.1 6.2 copy-start.13
  1128.1 6.2 copy-start.17
  1128.1 6.2 copy-start.20
  1132.9 261.6 %all-reduce.3.cloned.1.call-start = ((), (), s32[]{:S(2)}) async-start(), calls=%async_computation.24 | async-start | bytes 188416 | tf_op jit(solution)/shard_map/psum | solution.py:249
  1134.3 9.7 copy-start.30
  1134.3 9.7 copy-start.28
  1134.3 10.9 copy-start.9
  1144.0 3.2 copy-start.3
  1144.0 3.2 copy-start.6
  1144.0 3.2 copy-start.26
Sparse Core Ops, SparseCore 0:
  9.6 100.1 all-gather.12
  120.3 62.2 all-gather.16
  185.3 62.3 all-gather.14
  249.1 40.8 all-gather.18
  291.4 128.8 all-gather.20
  421.8 133.3 all-gather.22
  557.8 69.9 all-gather.24
  629.9 91.0 all-gather.30
  723.0 62.7 all-gather.32
  787.7 62.1 all-gather.26
  851.9 62.3 all-gather.28
  916.3 202.6 all-gather.34
  1121.6 23.4 reduce-scatter.8
  1147.5 36.1 reduce-scatter.10
  1186.0 30.8 reduce-scatter.6
  1219.4 38.7 reduce-scatter.12
  1265.6 128.8 all-reduce.2
where the time goes:
time: 1420 us; the launch traced here: 1410 us
  waiting for transfers between devices  970 us (68%)
  matrix products  189 us (13%)
  blocking collectives  102 us (7%)
  local copies, waits for them, and re-layouts  82.1 us (6%)
  other arithmetic  34.4 us (2%)
  starting transfers between devices  21.4 us (2%)
  between operations  14.8 us (1%)
    all_gather x4, waiting for transfers between devices, fetch(): return lax.all_gather(weight, 'fsdp', axis=0, tiled=True)  341 us
    all_gather x4, waiting for transfers between devices, column_grad(): whole_left = lax.all_gather(left, 'ctx', axis=0, tiled=True)  183 us
    psum x1, waiting for transfers between devices, body(): lax.psum((grad_query_bias, grad_value_bias, grad_out_bias, grad_expand_bi...  134 us
    all_gather x1, waiting for transfers between devices, body(): lax.all_gather(keys_own, 'ctx', axis=0, tiled=True)  57.6 us
    all_gather x1, waiting for transfers between devices, body(): lax.all_gather(grad_att_low, 'ctx', axis=0, tiled=True)  56.4 us
    all_gather x1, waiting for transfers between devices, body(): lax.all_gather(values_own, 'ctx', axis=0, tiled=True)  53.8 us
    reduce_scatter x3, waiting for transfers between devices, shard_rows(): lax.psum_scatter(local.astype(jnp.bfloat16), 'fsdp', scatter_dimension=0,...  52.4 us
    all_to_all x3, waiting for transfers between devices, column_grad(): lax.all_to_all(right, 'ctx', split_axis=1, concat_axis=0, tiled=True)  48.3 us
  transfers between devices with their start and end apart: 20, of which 14 were waited for; matrix products, arithmetic and copies ran while one was open for 20% of the time, Pallas kernels for 0%

commit v1 on v0

--- a/solution.py
+++ b/solution.py
@@ -41,7 +41,10 @@
 
 def column_grad(left, right):
     whole_left = lax.all_gather(left, "ctx", axis=0, tiled=True)
-    right_columns = lax.all_to_all(right, "ctx", split_axis=1, concat_axis=0, tiled=True)
+    right_columns = jnp.concatenate(
+        lax.all_to_all(jnp.stack(jnp.split(right, lax.axis_size("ctx"), axis=1)), "ctx", 0, 0),
+        axis=0,
+    )
     local = lax.dot_general(
         whole_left, right_columns, (((0,), (0,)), ((), ())), preferred_element_type=jnp.float32
     )

time: 1420 us -> 1420 us (level)
  local copies, waits for them, and re-layouts: 82.1 us -> 105 us
    unnamed x83 -> x117, local copies, waits for them, and re-layouts: 38 us -> 58.1 us
    all_gather x4, waiting for transfers between devices: 183 us -> 166 us  [column_grad(): whole_left = lax.all_gather(left, 'ctx', axis=0, tiled=True)]
  transfers between devices with their start and end apart: 20 -> 20, of which waited for: 14 -> 15; matrix products, arithmetic and copies ran while one was open for 20% -> 21% of each run, Pallas kernels for 0% -> 0%
where the time goes in v1:
time: 1420 us
  waiting for transfers between devices  960 us (68%)
  matrix products  189 us (13%)
  local copies, waits for them, and re-layouts  105 us (7%)
  blocking collectives  94.5 us (7%)
  other arithmetic  32.3 us (2%)
  starting transfers between devices  19.1 us (1%)
  between operations  15 us (1%)
    all_gather x4, waiting for transfers between devices, fetch(): return lax.all_gather(weight, 'fsdp', axis=0, tiled=True)  341 us
    all_gather x4, waiting for transfers between devices, column_grad(): whole_left = lax.all_gather(left, 'ctx', axis=0, tiled=True)  166 us
    psum x1, waiting for transfers between devices, body(): lax.psum((grad_query_bias, grad_value_bias, grad_out_bias, grad_expand_bi...  134 us
    unnamed x117, local copies, waits for them, and re-layouts  58.1 us
    all_gather x1, waiting for transfers between devices, body(): lax.all_gather(keys_own, 'ctx', axis=0, tiled=True)  57.6 us
    all_gather x1, waiting for transfers between devices, body(): lax.all_gather(grad_att_low, 'ctx', axis=0, tiled=True)  56.5 us
    all_gather x1, waiting for transfers between devices, body(): lax.all_gather(values_own, 'ctx', axis=0, tiled=True)  53.8 us
    reduce_scatter x3, waiting for transfers between devices, shard_rows(): lax.psum_scatter(local.astype(jnp.bfloat16), 'fsdp', scatter_dimension=0,...  53.5 us
  transfers between devices with their start and end apart: 20, of which 15 were waited for; matrix products, arithmetic and copies ran while one was open for 21% of the time, Pallas kernels for 0%

profile of v1, /device:TPU:8, one launch (start us, length us, event | category | flops | bytes accessed | tf_op | source)
XLA Modules:
  0.0 1415.7 jit_solution(6711984197787299136)
XLA Ops:
  9.8 100.0 %all-gather.13.cloned.1.call-done = bf16[1600,4800]{1,0:T(8,128)(2,1)} async-done(((bf16[400,4800]{1,0:T(8,128)(2,1)}), bf16[1600,4800]{1,0:T(8,128)(2,1)}) %all-gather.13.cloned.1.call-update) | async-done | bytes 15360016 | tf_op jit(solution)/shard_map/all_gather | solution.py:27
  109.8 9.6 fusion.196
  125.1 57.6 %all-gather.17.cloned.1.call-done = bf16[1024,1600]{0,1:T(8,128)(2,1)} async-done(((bf16[128,1600]{0,1:T(8,128)(2,1)}), bf16[1024,1600]{0,1:T(8,128)(2,1)}) %all-gather.17.cloned.1.call-update) | async-done | bytes 3276816 | tf_op jit(solution)/shard_map/all_gather | solution.py:102
  182.7 8.5 reshape.297
  191.2 2.7 copy.97
  193.9 53.8 %all-gather.15.cloned.1.call-done = bf16[1024,1600]{0,1:T(8,128)(2,1)} async-done(((bf16[128,1600]{0,1:T(8,128)(2,1)}), bf16[1024,1600]{0,1:T(8,128)(2,1)}) %all-gather.15.cloned.1.call-update) | async-done | bytes 3276816 | tf_op jit(solution)/shard_map/all_gather | solution.py:103
  247.7 8.5 reshape.296
  256.2 4.9 copy.96
  261.0 19.3 %while.48 = (s32[]{:T(128)}, f32[25,128]{1,0:T(8,128)S(1)}, f32[25,128]{1,0:T(8,128)S(1)}, s32[2,512]{1,0:T(2,128)S(1)}, s32[128]{0:T(128)S(1)}, /*index=5*/bf16...) while((s32[]{:T(128)}, f32[25,128]{1,0:T(8,128)S(1)}, ...), condition=%wide.region_5.6_spmd.clone, body=%wide.region_2.5_spmd.clone.sunk | while | flops 221265536 | bytes 15524976 | solution.py:121
  261.2 5.2 fusion.252
  266.4 4.3 exponential_reduce_fusion.2
  270.9 5.2 fusion.252
  276.1 4.2 exponential_reduce_fusion.2
  280.4 10.0 while.49
  280.5 4.7 fusion.258
  285.4 5.0 fusion.258
  292.7 5.0 fusion.195
  299.9 120.4 %all-gather.21.cloned.1.call-done = bf16[1600,6400]{1,0:T(8,128)(2,1)} async-done(((bf16[400,6400]{1,0:T(8,128)(2,1)}), bf16[1600,6400]{1,0:T(8,128)(2,1)}) %all-gather.21.cloned.1.call-update) | async-done | bytes 20480016 | tf_op jit(solution)/shard_map/all_gather | solution.py:27
  420.3 14.0 multiply_convert_fusion.6
  434.3 120.9 %all-gather.23.cloned.1.call-done = bf16[6400,1600]{1,0:T(8,128)(2,1)} async-done(((bf16[1600,1600]{1,0:T(8,128)(2,1)}), bf16[6400,1600]{1,0:T(8,128)(2,1)}) %all-gather.23.cloned.1.call-update) | async-done | bytes 20480016 | tf_op jit(solution)/shard_map/all_gather | solution.py:27
  555.2 12.7 convert_reduce_fusion
  567.9 12.8 multiply_reduce_fusion
  583.8 2.3 convolution_convert_fusion.4
  587.4 30.4 %all_gather.52 = f32[1024,25]{0,1:T(8,128)S(1)} all-gather(f32[128,25]{0,1:T(8,128)S(1)} %bitcast.486), channel_id=1, replica_groups=mesh['ctx'=8,'fsdp'=4] {'ctx'}, dimensions={0}, use_global_device_ids=true | all-gather | bytes 115200 | tf_op jit(solution)/shard_map/all_gather | solution.py:202
  618.6 3.5 all-gather.25.cloned.1.call-done
  622.1 8.5 reshape.300
  630.6 4.6 copy.100
  640.1 6.2 all-to-all-start.1
  660.3 3.7 copy.106
  665.4 6.0 all-to-all-start.2
  671.4 24.5 %while.50 = (s32[]{:T(128)}, f32[128,25,64]{0,2,1:T(8,128)}, bf16[2,512,25,64]{1,3,2,0:T(8,128)(2,1)S(1)}, s32[2,512]{1,0:T(2,128)S(1)}, s32[128]{0:T(128)S(1)},...) while((s32[]{:T(128)}, f32[128,25,64]{0,2,1:T(8,128)}, ...), condition=%wide.region_14.15_spmd.clone, body=%wide.region_13.14_spmd.clone.sunk | while | flops 639451136 | bytes 20651656 | solution.py:196
  671.6 4.7 fusion.265
  676.5 7.2 fusion.266
  683.7 4.7 fusion.265
  688.6 7.3 fusion.266
  695.9 19.7 %all-gather.31.cloned.1.call-done = bf16[1024,1600]{0,1:T(8,128)(2,1)} async-done(((bf16[128,1600]{0,1:T(8,128)(2,1)}), bf16[1024,1600]{0,1:T(8,128)(2,1)}) %all-gather.31.cloned.1.call-update) | async-done | bytes 3276816 | tf_op jit(solution)/shard_map/all_gather | solution.py:43
  715.6 3.9 convolution_convert_fusion.3
  719.9 35.4 %all_gather.54 = f32[1024,25]{0,1:T(8,128)S(1)} all-gather(f32[128,25]{0,1:T(8,128)S(1)} %bitcast.485), channel_id=1, replica_groups=mesh['ctx'=8,'fsdp'=4] {'ctx'}, dimensions={0}, use_global_device_ids=true | all-gather | bytes 115200 | tf_op jit(solution)/shard_map/all_gather | solution.py:203
  757.4 27.0 %all-gather.33.cloned.1.call-done = bf16[1024,1600]{0,1:T(8,128)(2,1)} async-done(((bf16[128,1600]{0,1:T(8,128)(2,1)}), bf16[1024,1600]{0,1:T(8,128)(2,1)}) %all-gather.33.cloned.1.call-update) | async-done | bytes 3276816 | tf_op jit(solution)/shard_map/all_gather | solution.py:43
  784.4 7.6 convolution_convert_fusion.1
  792.1 56.5 %all-gather.27.cloned.1.call-done = bf16[1024,1600]{0,1:T(8,128)(2,1)} async-done(((bf16[128,1600]{0,1:T(8,128)(2,1)}), bf16[1024,1600]{0,1:T(8,128)(2,1)}) %all-gather.27.cloned.1.call-update) | async-done | bytes 3276816 | tf_op jit(solution)/shard_map/all_gather | solution.py:199
  848.6 8.7 reshape.303
  857.3 4.8 copy.102
  862.1 41.7 %while.51 = (s32[]{:T(128)}, f32[128,25,64]{0,2,1:T(8,128)}, f32[128,25,64]{0,2,1:T(8,128)}, bf16[2,512,25,64]{1,3,2,0:T(8,128)(2,1)S(1)}, s32[128]{0:T(128)S(1)...) while((s32[]{:T(128)}, f32[128,25,64]{0,2,1:T(8,128)}, ...), condition=%wide.region_16.17_spmd.clone, body=%wide.region_15.16_spmd.clone.sunk | while | flops 856129536 | bytes 31107220 | solution.py:228
  862.1 4.7 fusion.274
  868.1 9.1 fusion.275
  877.2 5.6 fusion.276
  882.7 4.8 fusion.274
  888.7 9.2 fusion.275
  898.0 5.8 fusion.276
  910.6 5.8 all-to-all-start
  916.4 50.2 %all-to-all-done = bf16[8,128,600]{1,2,0:T(8,128)(2,1)S(1)} async-done(((bf16[8,128,600]{1,2,0:T(8,128)(2,1)}), bf16[8,128,600]{1,2,0:T(8,128)(2,1)S(1)}, u32[]{:S(2)}, u32[]{:S(2)}) %all-to-all-start) | async-done | bytes 1228832 | tf_op jit(solution)/shard_map/all_to_all | solution.py:45
  966.6 6.0 convolution_convert_fusion.2
  972.8 28.7 %all_to_all.20 = bf16[8,128,200]{1,2,0:T(8,128)(2,1)S(1)} all-to-all(bf16[8,128,200]{1,2,0:T(8,128)(2,1)S(1)} %constant_dynamic-update-slice_fusion.8), channel_id=1, replica_groups=mesh['ctx'=8,'fsdp'=4] {'ctx'}, dimensions={0} | all-to-all | bytes 819200 | tf_op jit(solution)/shard_map/all_to_all | solution.py:45
  1001.5 119.4 %all-gather.35.cloned.1.call-done = bf16[1024,6400]{1,0:T(8,128)(2,1)} async-done(((bf16[128,6400]{1,0:T(8,128)(2,1)}), bf16[1024,6400]{1,0:T(8,128)(2,1)}) %all-gather.35.cloned.1.call-update) | async-done | bytes 13107216 | tf_op jit(solution)/shard_map/all_gather | solution.py:43
  1120.9 9.0 convolution_convert_fusion
  1129.9 4.8 copy.111
  1135.5 13.3 fusion.136
  1151.3 9.8 fusion.192
  1163.6 22.4 %reduce-scatter.11.cloned.1.call-done = bf16[400,800]{1,0:T(8,128)(2,1)} async-done(((bf16[1600,800]{1,0:T(8,128)(2,1)}), bf16[400,800]{1,0:T(8,128)(2,1)}) %reduce-scatter.11.cloned.1.call-update) | async-done | bytes 640016 | tf_op jit(solution)/shard_map/reduce_scatter | solution.py:37
  1186.0 2.3 convert_element_type.142
  1188.3 31.0 %reduce-scatter.7.cloned.1.call-done = bf16[400,600]{1,0:T(8,128)(2,1)} async-done(((bf16[1600,600]{1,0:T(8,128)(2,1)}), bf16[400,600]{1,0:T(8,128)(2,1)}) %reduce-scatter.7.cloned.1.call-update) | async-done | bytes 480016 | tf_op jit(solution)/shard_map/reduce_scatter | solution.py:37
  1221.4 39.1 %reduce-scatter.13.cloned.1.call-done = bf16[1600,200]{1,0:T(8,128)(2,1)} async-done(((bf16[6400,200]{1,0:T(8,128)(2,1)}), bf16[1600,200]{1,0:T(8,128)(2,1)}) %reduce-scatter.13.cloned.1.call-update) | async-done | bytes 640016
  1263.2 133.8 %all-reduce.3.cloned.1.call-done = (f32[1600]{0:T(1024)}, f32[1600]{0:T(1024)}, f32[1600]{0:T(1024)}, f32[6400]{0:T(1024)}, f32[1600]{0:T(1024)}, /*index=5*/f32...) async-done(((f32[1600]{0:T(1024)}, f32[1600]{0:T(1024)}, f32[1600]{0:T(1024)}, f32[6400]{0:T(1024)}, f32[1600]{0:T(1024)}, /*index=5*/f32[1600]{0:T(1024)}, ...) | async-done | bytes 76816 | tf_op jit(solution)/shard_map/psum | solution.py:252
  (233 shorter events, 72.6 us)
Async XLA Ops:
  7.2 1.0 copy-start.4
  7.2 2.0 copy-start.20
  7.2 2.0 copy-start.25
  7.2 102.6 %all-gather.13.cloned.1.call-start = ((), (), s32[]{:S(2)}) async-start(), calls=%async_computation.8 | async-start | bytes 19456000 | tf_op jit(solution)/shard_map/all_gather | solution.py:27
  7.9 174.7 %all-gather.17.cloned.1.call-start = ((), (), s32[]{:S(2)}) async-start(), calls=%async_computation.10 | async-start | bytes 3686400 | tf_op jit(solution)/shard_map/all_gather | solution.py:102
  8.4 1.3 copy-start.23
  8.7 0.6 copy-start.33
  9.2 0.5 copy-start.31
  9.7 109.6 %copy-start.13 = (bf16[128,1600]{0,1:T(8,128)(2,1)}, bf16[128,1600]{0,1:T(8,128)(2,1)S(1)}, u32[]{:S(2)}) copy-start(bf16[128,1600]{0,1:T(8,128)(2,1)S(1)} %fusion.155) | copy-start | bytes 1228804
  9.8 110.5 %copy-start.26 = (f32[1600]{0:T(1024)S(1)}, f32[1600]{0:T(1024)}, u32[]{:S(2)}) copy-start(f32[1600]{0:T(1024)} %param.27) | copy-start | bytes 19204
  9.8 110.5 %copy-start.27 = (f32[1600]{0:T(1024)S(1)}, f32[1600]{0:T(1024)}, u32[]{:S(2)}) copy-start(f32[1600]{0:T(1024)} %param.28) | copy-start | bytes 19204
  120.2 127.5 %all-gather.15.cloned.1.call-start = ((), (), s32[]{:S(2)}) async-start(), calls=%async_computation.9 | async-start | bytes 3686400 | tf_op jit(solution)/shard_map/all_gather | solution.py:103
  121.7 171.0 %all-gather.19.cloned.1.call-start = ((), (), s32[]{:S(2)}) async-start(), calls=%async_computation.11 | async-start | bytes 6656000 | tf_op jit(solution)/shard_map/all_gather | solution.py:27
  122.3 298.1 %all-gather.21.cloned.1.call-start = ((), (), s32[]{:S(2)}) async-start(), calls=%async_computation.12 | async-start | bytes 25600000 | tf_op jit(solution)/shard_map/all_gather | solution.py:27
  122.9 1.6 copy-start.35
  122.9 432.3 %all-gather.23.cloned.1.call-start = ((), (), s32[]{:S(2)}) async-start(), calls=%async_computation.13 | async-start | bytes 26624000 | tf_op jit(solution)/shard_map/all_gather | solution.py:27
  123.5 498.7 %all-gather.25.cloned.1.call-start = ((), (), s32[]{:S(2)}) async-start(), calls=%async_computation.14 | async-start | bytes 3686400 | tf_op jit(solution)/shard_map/all_gather | solution.py:198
  124.2 591.4 %all-gather.31.cloned.1.call-start = ((), (), s32[]{:S(2)}) async-start(), calls=%async_computation.18 | async-start | bytes 3686400 | tf_op jit(solution)/shard_map/all_gather | solution.py:43
  280.3 12.4 copy-start.28
  292.4 6.2 copy-start.19
  292.4 6.2 copy-start.29
  292.4 128.0 %copy-start.22 = (f32[6400]{0:T(1024)S(1)}, f32[6400]{0:T(1024)}, u32[]{:S(2)}) copy-start(f32[6400]{0:T(1024)} %param.32) | copy-start | bytes 76804
  292.4 492.0 %all-gather.33.cloned.1.call-start = ((), (), s32[]{:S(2)}) async-start(), calls=%async_computation.20 | async-start | bytes 3686400 | tf_op jit(solution)/shard_map/all_gather | solution.py:43
  297.7 0.9 copy-start.1
  299.9 548.7 %all-gather.27.cloned.1.call-start = ((), (), s32[]{:S(2)}) async-start(), calls=%async_computation.15 | async-start | bytes 3686400 | tf_op jit(solution)/shard_map/all_gather | solution.py:199
  555.2 12.7 copy-start.2
  567.9 12.8 copy-start.7
  567.9 15.8 %slice-start = ((s8[5324800]{0:T(1024)(128)(4,1)}), s8[4194304]{0:T(1024)(128)(4,1)S(1)}, s32[]{:S(2)}) async-start(s8[5324800]{0:T(1024)(128)(4,1)} %bitcast.454), calls=%async_computation.25 | async-start | bytes 8388608
  567.9 14.0 copy-start.10
  567.9 15.8 %slice-start.1 = ((s8[5324800]{0:T(1024)(128)(4,1)}), s8[1130496]{0:T(1024)(128)(4,1)S(1)}, s32[]{:S(2)}) async-start(s8[5324800]{0:T(1024)(128)(4,1)} %bitcast.454), calls=%async_computation.26 | async-start | bytes 2260992
  581.1 0.9 copy-start.8
  583.0 0.7 copy-start.16
  586.1 330.3 %all-gather.29.cloned.1.call-start = ((), (), s32[]{:S(2)}) async-start(), calls=%async_computation.16 | async-start | bytes 3686400 | tf_op jit(solution)/shard_map/all_gather | solution.py:43
  586.8 534.0 %all-gather.35.cloned.1.call-start = ((), (), s32[]{:S(2)}) async-start(), calls=%async_computation.22 | async-start | bytes 14745600 | tf_op jit(solution)/shard_map/all_gather | solution.py:43
  630.6 4.6 copy-start.17
  640.1 25.3 %all-to-all-start.1 = ((bf16[8,128,200]{1,2,0:T(8,128)(2,1)}), bf16[8,128,200]{1,2,0:T(8,128)(2,1)}, u32[]{:S(2)}, u32[]{:S(2)}) async-start(bf16[8,128,200]{1,2,0:T(8,128)(2,1)} %constant_dynamic-update-slice_fusion), calls=%async_computation.2 | async-start | bytes 819200 | tf_op jit(solution)/shard_map/all_to_all | solution.py:45
  665.4 92.0 %all-to-all-start.2 = ((bf16[8,128,800]{1,2,0:T(8,128)(2,1)}), bf16[8,128,800]{1,2,0:T(8,128)(2,1)}, u32[]{:S(2)}, u32[]{:S(2)}) async-start(bf16[8,128,800]{1,2,0:T(8,128)(2,1)} %copy.106), calls=%async_computation.4 | async-start | bytes 3276800 | tf_op jit(solution)/shard_map/all_to_all | solution.py:45
  671.4 477.4 %reduce-scatter.9.cloned.1.call-start = ((), (), s32[]{:S(2)}) async-start(), calls=%async_computation.19 | async-start | bytes 1024000 | tf_op jit(solution)/shard_map/reduce_scatter | solution.py:37
  695.9 23.7 %copy-start.18 = (f32[128,25,64]{0,2,1:T(8,128)S(1)}, f32[128,25,64]{0,2,1:T(8,128)}, u32[]{:S(2)}) copy-start(f32[128,25,64]{0,2,1:T(8,128)} %get-tuple-element.208) | copy-start | bytes 2457604
  719.5 466.5 %reduce-scatter.11.cloned.1.call-start = ((), (), s32[]{:S(2)}) async-start(), calls=%async_computation.21 | async-start | bytes 3584000 | tf_op jit(solution)/shard_map/reduce_scatter | solution.py:37
  719.9 72.1 %copy-start.15 = (bf16[128,25,64]{0,2,1:T(8,128)(2,1)}, bf16[128,25,64]{0,2,1:T(8,128)(2,1)S(1)}, u32[]{:S(2)}) copy-start(bf16[128,25,64]{0,2,1:T(8,128)(2,1)S(1)} %get-tuple-element.604) | copy-start | bytes 1228804
  857.3 4.8 copy-start
  905.5 4.4 copy-start.14
  910.6 56.0 %all-to-all-start = ((bf16[8,128,600]{1,2,0:T(8,128)(2,1)}), bf16[8,128,600]{1,2,0:T(8,128)(2,1)S(1)}, u32[]{:S(2)}, u32[]{:S(2)}) async-start(bf16[8,128,600]{1,2,0:T(8,128)(2,1)} %fusion.174), calls=%async_computation | async-start | bytes 2457600 | tf_op jit(solution)/shard_map/all_to_all | solution.py:45
  916.4 56.3 %copy-start.11 = (bf16[1,128,1600]{1,2,0:T(8,128)(2,1)S(1)}, bf16[1,128,1600]{1,2,0:T(8,128)(2,1)}, u32[]{:S(2)}) copy-start(bf16[1,128,1600]{1,2,0:T(8,128)(2,1)} %param.39) | copy-start | bytes 1228804
  916.4 302.9 %reduce-scatter.7.cloned.1.call-start = ((), (), s32[]{:S(2)}) async-start(), calls=%async_computation.17 | async-start | bytes 2560000 | tf_op jit(solution)/shard_map/reduce_scatter | solution.py:37
  972.6 287.9 %reduce-scatter.13.cloned.1.call-start = ((), (), s32[]{:S(2)}) async-start(), calls=%async_computation.23 | async-start | bytes 4096000
  1129.9 5.6 copy-start.3
  1129.9 5.6 copy-start.6
  1129.9 5.6 copy-start.30
  1134.8 262.2 %all-reduce.3.cloned.1.call-start = ((), (), s32[]{:S(2)}) async-start(), calls=%async_computation.24 | async-start | bytes 188416 | tf_op jit(solution)/shard_map/psum | solution.py:252
  1135.5 15.8 %copy-start.5 = (bf16[1,128,1600]{1,2,0:T(8,128)(2,1)S(1)}, bf16[1,128,1600]{1,2,0:T(8,128)(2,1)}, u32[]{:S(2)}) copy-start(bf16[1,128,1600]{1,2,0:T(8,128)(2,1)} %param.24) | copy-start | bytes 1228804
  1135.5 15.8 %copy-start.21 = (f32[1600]{0:T(1024)S(1)}, f32[1600]{0:T(1024)}, u32[]{:S(2)}) copy-start(f32[1600]{0:T(1024)} %param.35) | copy-start | bytes 19204
  1135.5 15.7 %copy-start.24 = (f32[128]{0:T(128)S(1)}, f32[128]{0:T(128)}, u32[]{:S(2)}) copy-start(f32[128]{0:T(128)} %copy-done.23) | copy-start | bytes 1540
  1151.2 9.8 copy-start.34
  1151.3 9.9 copy-start.32
  1151.3 11.0 copy-start.9
  1151.3 11.0 copy-start.12
Sparse Core Ops, SparseCore 0:
  9.6 100.1 all-gather.12
  120.3 62.2 all-gather.16
  185.3 62.3 all-gather.14
  249.1 40.8 all-gather.18
  291.4 128.8 all-gather.20
  421.8 133.3 all-gather.22
  557.8 64.2 all-gather.24
  624.1 91.3 all-gather.30
  717.6 66.7 all-gather.32
  786.3 62.2 all-gather.26
  850.6 62.3 all-gather.28
  915.1 205.7 all-gather.34
  1124.0 23.4 reduce-scatter.8
  1149.8 36.1 reduce-scatter.10
  1188.4 30.8 reduce-scatter.6
  1221.8 38.7 reduce-scatter.12
  1268.0 128.9 all-reduce.2
